TPU v7x, 32 devices: a whole 2x2x4 slice. The times are simulated.
32 devices in a mesh: dp: 8 (over z, x), hyper: 4 (over y, core).
Axes of the slice: x: 2, y: 2, z: 4, core: 2. Of those that a mesh axis runs over, the one named last changes fastest.
Arguments:
- inputs: bfloat16 [64, 64, 128], P(('dp', 'hyper')), may hold values from -64 to 64
- labels: int32 [64, 64], P(('dp', 'hyper')), may hold values from 0 to 255
- client_ids: int32 [64], P(('dp', 'hyper')), may hold values from 0 to 63
- ext_weight: bfloat16 [128, 4096], replicated, may hold values from -0.5 to 0.5
- ext_bias: bfloat16 [4096], replicated, may hold values from -3 to 3
- embeddings: bfloat16 [64, 128], replicated, may hold values from -1.5 to 1.5
- hyper_in: bfloat16 [128, 50], replicated, may hold values from -2.09375 to 2.09375
- hyper_bias: float32 [50], replicated, may hold values from -3 to 3
- hyper_out: bfloat16 [4096, 50, 256], P('hyper'), may hold values from -0.1796875 to 0.1796875
Outputs:
- grad_ext_weight: float32 [128, 4096], replicated
- grad_ext_bias: float32 [4096], replicated
- grad_embeddings: float32 [64, 128], replicated
- grad_hyper_in: float32 [128, 50], replicated
- grad_hyper_bias: float32 [50], replicated
- grad_hyper_out: float32 [4096, 50, 256], P(('hyper', 'dp'))
Inputs may be any that keep to these rules, and one draw needn't show every extreme that they name: `client_ids`: A client may hold several slots or none.
All inputs are finite; a program needn't handle non-finite values.
Results may differ from a plain program's by a relative error of at most 0.014.
The roundings to bfloat16 on the way count: a program that leaves them out, or rounds other values in their place, can miss the bound.
Values may be sent and summed in bfloat16 or wider, within the bound.
A program may use at most 192 MiB of HBM per device.

v0:
```python
import jax
import jax.numpy as jnp
from jax import lax
from jax.sharding import PartitionSpec as P

highest = lax.Precision.HIGHEST
f32 = jnp.float32
bf16 = jnp.bfloat16


def silu_slope(values):
    logistic = jax.nn.sigmoid(values)
    return logistic * (1.0 + values * (1.0 - logistic))


def class_grads(logits, slot_labels, row_count):
    largest = jnp.max(logits, axis=-1, keepdims=True)
    exponent = jnp.exp(logits - largest)
    probability = exponent / jnp.sum(exponent, axis=-1, keepdims=True)
    classes = jnp.arange(logits.shape[-1], dtype=jnp.int32)
    onehot = (slot_labels[..., None] == classes).astype(f32)
    return ((probability - onehot) / row_count).astype(bf16)


def local(
    inputs, labels, client_ids, ext_weight, ext_bias, embeddings, hyper_in, hyper_bias, hyper_out
):
    everyone = ("dp", "hyper")
    n_dp, n_hyper = (lax.axis_size("dp"), lax.axis_size("hyper"))
    i, j = (lax.axis_index("dp"), lax.axis_index("hyper"))
    own, rows, width_in = inputs.shape
    wide = hyper_out.shape[0]
    narrow = wide // n_dp
    group = own * n_hyper
    slots = group * n_dp
    classes = hyper_out.shape[2]
    ids = lax.all_gather(client_ids, everyone, axis=0, tiled=True)
    in_group = lax.all_gather(inputs, "hyper", axis=0, tiled=True)
    in_all = lax.all_gather(in_group, "dp", axis=0, tiled=True)
    select = ids[:, None] == jnp.arange(embeddings.shape[0], dtype=jnp.int32)[None, :]
    picked = jnp.dot(select.astype(bf16), embeddings, preferred_element_type=f32).astype(bf16)
    hyper_preact = jnp.dot(picked, hyper_in, preferred_element_type=f32) + hyper_bias
    hidden = jax.nn.silu(hyper_preact).astype(bf16)
    w_wide = lax.dynamic_slice_in_dim(ext_weight, j * wide, wide, 1)
    b_wide = lax.dynamic_slice_in_dim(ext_bias, j * wide, wide, 0).astype(f32)
    preact = jnp.dot(in_group.reshape(group * rows, width_in), w_wide, preferred_element_type=f32)
    features = jax.nn.silu(preact + b_wide).astype(bf16).reshape(group, rows, wide)
    hidden_group = lax.dynamic_slice_in_dim(hidden, i * group, group, 0)
    heads = jnp.einsum("kh,dhc->kdc", hidden_group, hyper_out, preferred_element_type=f32)
    part = jnp.einsum("krd,kdc->krc", features, heads.astype(bf16), preferred_element_type=f32)
    parts = lax.all_to_all(
        part.reshape(n_hyper, own * rows, classes), "hyper", split_axis=0, concat_axis=0
    )
    logits = jnp.sum(parts, axis=0).reshape(own, rows, classes)
    dlogits = class_grads(logits, labels, rows)
    dl_all = lax.all_gather(dlogits, everyone, axis=0, tiled=True)
    start = (j * n_dp + i) * narrow
    w = lax.dynamic_slice_in_dim(ext_weight, start, narrow, 1)
    b = lax.dynamic_slice_in_dim(ext_bias, start, narrow, 0).astype(f32)
    out_rows = lax.dynamic_slice_in_dim(hyper_out, i * narrow, narrow, 0)
    flat = in_all.reshape(slots * rows, width_in)
    preact = jnp.dot(flat, w, preferred_element_type=f32) + b
    features = jax.nn.silu(preact).astype(bf16).reshape(slots, rows, narrow)
    heads = jnp.einsum("kh,dhc->kdc", hidden, out_rows, preferred_element_type=f32).astype(bf16)
    dheads = jnp.einsum("krd,krc->kdc", features, dl_all, preferred_element_type=f32).astype(bf16)
    dfeatures = jnp.einsum("krc,kdc->krd", dl_all, heads, preferred_element_type=f32).astype(bf16)
    dpreact = (dfeatures.reshape(slots * rows, narrow).astype(f32) * silu_slope(preact)).astype(
        bf16
    )
    grad_weight = jnp.dot(flat.T, dpreact, preferred_element_type=f32)
    grad_bias = jnp.sum(dpreact.astype(f32), axis=0)
    grad_out = jnp.einsum("kh,kdc->dhc", hidden, dheads, preferred_element_type=f32)
    dhidden = jnp.einsum("kdc,dhc->kh", dheads, out_rows, preferred_element_type=f32)
    dhidden = lax.psum(dhidden, everyone)
    hyper_dpre = dhidden * silu_slope(hyper_preact)
    grad_in = jnp.dot(picked.astype(f32).T, hyper_dpre, precision=highest)
    grad_hbias = jnp.sum(hyper_dpre, axis=0)
    back_rows = jnp.dot(hyper_dpre, hyper_in.astype(f32).T, precision=highest)
    grad_table = jnp.dot(select.astype(f32).T, back_rows, precision=highest)
    both = jnp.concatenate([grad_weight, grad_bias[None]], axis=0)
    both = lax.all_gather(both, ("hyper", "dp"), axis=1, tiled=True)
    return (both[:-1], both[-1], grad_table, grad_in, grad_hbias, grad_out)


def solution(mesh):
    placed = (
        P(("dp", "hyper"), None, None),
        P(("dp", "hyper"), None),
        P(("dp", "hyper")),
        P(),
        P(),
        P(),
        P(),
        P(),
        P("hyper", None, None),
    )
    return jax.shard_map(
        local,
        mesh=mesh,
        in_specs=placed,
        out_specs=(P(), P(), P(), P(), P(), P(("hyper", "dp"), None, None)),
        check_vma=False,
    )
```

profile of v0, /device:TPU:0, one launch (start us, length us, event | category | flops | bytes accessed | tf_op | source)
XLA Modules:
  0.0 276.0 jit_solution(7571744221663631513)
XLA Ops:
  7.2 0.9 dynamic-update-slice
  8.2 42.0 %all-reduce = s32[64]{0:T(128)S(1)} all-reduce(s32[64]{0:T(128)S(1)} %dynamic-update-slice), channel_id=1, replica_groups=mesh['dp'=8,'hyper'=4] {'dp','hyper'}, use_global_device_ids=true, to_apply=%add | all-reduce | flops 64 | bytes 512
  50.1 6.0 %all_gather.15 = bf16[8,64,128]{2,1,0:T(8,128)(2,1)S(1)} all-gather(bf16[2,64,128]{2,1,0:T(8,128)(2,1)} %param.9), channel_id=1, replica_groups=mesh['dp'=8,'hyper'=4] {'hyper'}, dimensions={0}, use_global_device_ids=true | all-gather | bytes 163840 | tf_op jit(solution)/shard_map/all_gather | solution.py:38
  56.1 0.7 dynamic-slice_convert_fusion
  56.8 0.9 convolution_convert_fusion.2
  57.7 0.9 multiply_convert_fusion.3
  58.6 0.7 fusion.21
  59.4 28.0 %convolution_convert_fusion.1 = bf16[8,1024,256]{2,0,1:T(8,128)(2,1)S(1)} fusion(bf16[64,50]{0,1:T(8,128)(2,1)S(1)} %get-tuple-element.29, s32[]{:T(128)S(6)} %select_n.15, bf16[1024,50,256]{2,0,1:T(8,128)(2,1)} %param.17), kind=kOutput, calls=%fused_computation.16 | convolution fusion | flops 211812352 | bytes 30415108 | tf_op jit(solution)/shard_map/kh,dhc->kdc/dot_general | solution.py:49
  87.4 0.9 fusion.3
  88.2 11.8 %all_to_all.5 = f32[4,128,256]{2,1,0:T(8,128)S(1)} all-to-all(f32[4,128,256]{2,1,0:T(8,128)S(1)} %bitcast.61), channel_id=1, replica_groups=mesh['dp'=8,'hyper'=4] {'hyper'}, dimensions={0} | all-to-all | bytes 1048576 | tf_op jit(solution)/shard_map/all_to_all | solution.py:51
  100.5 0.8 multiply_convert_fusion.2
  101.3 0.7 all-gather.6.cloned.1.call-update
  102.1 27.8 %copy.28 = bf16[1024,50,256]{2,1,0:T(8,128)(2,1)} copy(bf16[1024,50,256]{2,0,1:T(8,128)(2,1)} %param.17) | data formatting | bytes 52428800 | tf_op args[8]
  129.9 0.8 dynamic-slice_convert_fusion.1
  130.6 5.3 %fusion.15 = bf16[64,128,256]{2,0,1:T(8,128)(2,1)} fusion(bf16[1024,50,256]{2,1,0:T(8,128)(2,1)} %copy.28, s32[]{:T(128)S(6)} %select_n.16, bf16[64,50]{0,1:T(8,128)(2,1)S(1)} %get-tuple-element.29), kind=kOutput, calls=%fused_computation.14 | convolution fusion | flops 211812352 | bytes 7870724 | tf_op jit(solution)/shard_map/kh,dhc->kdc/dot_general | solution.py:64
  136.0 20.6 %all-gather.4.cloned.1.call-done = bf16[64,64,256]{2,1,0:T(8,128)(2,1)} async-done(((bf16[2,64,256]{2,1,0:T(8,128)(2,1)}), bf16[64,64,256]{2,1,0:T(8,128)(2,1)}) %all-gather.4.cloned.1.call-update) | async-done | bytes 2097168 | tf_op jit(solution)/shard_map/all_gather | solution.py:56
  156.5 5.5 %fusion.22 = bf16[64,64,128]{2,1,0:T(8,128)(2,1)S(1)} fusion(bf16[64,64,256]{2,1,0:T(8,128)(2,1)} %all-gather.4.cloned.1.call-done, bf16[64,128,256]{2,0,1:T(8,128)(2,1)} %fusion.15), kind=kOutput, calls=%fused_computation.27 | convolution fusion | flops 268959744 | bytes 7340032 | tf_op jit(solution)/shard_map/krc,kdc->krd/dot_general | solution.py:66
  162.3 1.8 copy.32
  164.1 33.7 %all-gather.6.cloned.1.call-done = bf16[64,64,128]{2,1,0:T(8,128)(2,1)} async-done(((bf16[8,64,128]{2,1,0:T(8,128)(2,1)}), bf16[64,64,128]{2,1,0:T(8,128)(2,1)}) %all-gather.6.cloned.1.call-update) | async-done | bytes 1048592 | tf_op jit(solution)/shard_map/all_gather | solution.py:39
  197.8 4.2 %convert_reduce_fusion = (f32[128]{0:T(128)S(1)}, bf16[4096,128]{0,1:T(8,128)(2,1)S(1)}, bf16[4096,128]{0,1:T(8,128)(2,1)}) fusion(f32[4096,128]{0,1:T(8,128)} %copy.32, f32[128]{0:T(128)S(1)} %dynamic-slice_convert_fusion.1, bf16[4096,128]{1,0:T(8,128)(2,1)} %bitcast.58, bf16[128,4096]{1,0:T(8,128)(2,1)S(1)} %copy-done, s32[]{:T(128)S(6)} %select_n.17), kind=kOutput, calls=%fused_computation.23 | convolution fusion | flops 141557632 | bytes 5276676 | tf_op jit(solution)/shard_map/dot_general | solution.py:62
  202.6 0.6 pad_maximum_fusion
  203.2 2.3 copy.33
  205.5 2.5 convolution_convert_fusion
  208.0 3.3 %fusion.12 = f32[128,50,256]{2,1,0:T(8,128)S(1)} fusion(bf16[64,128,256]{2,1,0:T(8,128)(2,1)S(1)} %convolution_convert_fusion, bf16[64,50]{0,1:T(8,128)(2,1)S(1)} %get-tuple-element.29), kind=kOutput, calls=%fused_computation.13 | convolution fusion | flops 209715200 | bytes 10754304 | tf_op jit(solution)/shard_map/kh,kdc->dhc/dot_general | solution.py:72
  211.3 4.8 %copy.37 = f32[128,50,256]{2,0,1:T(8,128)} copy(f32[128,50,256]{2,1,0:T(8,128)S(1)} %fusion.12) | data formatting | bytes 13107200
  216.1 7.1 %fusion.25 = f32[64,50]{0,1:T(8,128)S(1)} fusion(bf16[1024,50,256]{2,1,0:T(8,128)(2,1)} %copy.28, s32[]{:T(128)S(6)} %select_n.16, bf16[64,128,256]{2,1,0:T(8,128)(2,1)S(1)} %convolution_convert_fusion), kind=kOutput, calls=%fused_computation.29 | convolution fusion | flops 209715200 | bytes 7877124 | tf_op jit(solution)/shard_map/kdc,dhc->kh/dot_general | solution.py:73
  223.2 39.1 %psum.7 = f32[64,50]{0,1:T(8,128)S(1)} all-reduce(f32[64,50]{0,1:T(8,128)S(1)} %fusion.25), channel_id=1, replica_groups=mesh['dp'=8,'hyper'=4] {'dp','hyper'}, use_global_device_ids=true, to_apply=%region_4.5 | all-reduce | flops 3200 | bytes 25600 | tf_op jit(solution)/shard_map/psum | solution.py:74
  262.3 0.6 fusion.45
  263.2 0.9 fusion.32
  264.1 0.8 fusion.47
  264.9 1.5 slice.9
  266.4 3.1 %slice.8 = f32[128,4096]{1,0:T(8,128)} slice(f32[129,4096]{1,0:T(8,128)} %all-gather.8.cloned.1.call-done), slice={[0:128], [0:4096]} | slice | bytes 4194304 | tf_op jit(solution)/shard_map/slice | solution.py:82
  (27 shorter events, 1.6 us)
Async XLA Ops:
  7.2 51.5 %copy-start = (bf16[128,4096]{1,0:T(8,128)(2,1)S(1)}, bf16[128,4096]{1,0:T(8,128)(2,1)}, u32[]{:S(2)}) copy-start(bf16[128,4096]{1,0:T(8,128)(2,1)} %param.12) | copy-start | bytes 3145732
  7.2 149.4 %all-gather.4.cloned.1.call-start = ((), (), s32[]{:S(2)}) async-start(), calls=%async_computation.1 | async-start | bytes 2162688 | tf_op jit(solution)/shard_map/all_gather | solution.py:56
  56.1 3.2 %copy-start.3 = (bf16[8,64,128]{2,1,0:T(8,128)(2,1)}, bf16[8,64,128]{2,1,0:T(8,128)(2,1)S(1)}, u32[]{:S(2)}) copy-start(bf16[8,64,128]{2,1,0:T(8,128)(2,1)S(1)} %all_gather.15) | copy-start | bytes 393220
  87.4 13.1 %copy-start.5 = (s32[2,64]{1,0:T(2,128)S(1)}, s32[2,64]{1,0:T(2,128)}, u32[]{:S(2)}) copy-start(s32[2,64]{1,0:T(2,128)} %param.10) | copy-start | bytes 1540
  101.3 96.5 %all-gather.6.cloned.1.call-start = ((), (), s32[]{:S(2)}) async-start(), calls=%async_computation.2 | async-start | bytes 1179648 | tf_op jit(solution)/shard_map/all_gather | solution.py:39
  102.0 162.8 %all-gather.8.cloned.1.call-start = ((), (), s32[]{:S(2)}) async-start(), calls=%async_computation.3 | async-start | bytes 2297856 | tf_op jit(solution)/shard_map/all_gather | solution.py:81
  197.8 4.2 %copy-start.2 = (bf16[64,64,128]{2,1,0:T(8,128)(2,1)S(1)}, bf16[64,64,128]{2,1,0:T(8,128)(2,1)}, u32[]{:S(2)}) copy-start(bf16[64,64,128]{2,1,0:T(8,128)(2,1)} %all-gather.6.cloned.1.call-done) | copy-start | bytes 3145732
  202.1 3.4 %copy-start.1 = (bf16[64,64,256]{2,1,0:T(8,128)(2,1)S(1)}, bf16[64,64,256]{2,1,0:T(8,128)(2,1)}, u32[]{:S(2)}) copy-start(bf16[64,64,256]{2,1,0:T(8,128)(2,1)} %all-gather.4.cloned.1.call-done) | copy-start | bytes 6291460
  216.1 46.9 %copy-start.4 = (bf16[128,50]{0,1:T(8,128)(2,1)S(1)}, bf16[128,50]{0,1:T(8,128)(2,1)}, u32[]{:S(2)}) copy-start(bf16[128,50]{0,1:T(8,128)(2,1)} %param.15) | copy-start | bytes 38404
Sparse Core Ops, SparseCore 0:
  101.4 55.0 all-gather.3
  158.7 39.1 all-gather.5
  203.4 56.2 all-gather.7
where the time goes:
time: 277 us; the launch traced here: 276 us
  blocking collectives  98.8 us (36%)
  matrix products  61.7 us (22%)
  waiting for transfers between devices  55.1 us (20%)
  local copies, waits for them, and re-layouts  42.4 us (15%)
  between operations  13.9 us (5%)
  other arithmetic  4 us (1%)
    unnamed x1, blocking collectives  42 us
    psum x1, blocking collectives, local(): dhidden = lax.psum(dhidden, everyone)  39.1 us
    all_gather x1, waiting for transfers between devices, local(): in_all = lax.all_gather(in_group, 'dp', axis=0, tiled=True)  33.7 us
    unnamed x16, local copies, waits for them, and re-layouts  33.5 us
    dot_general x1, matrix products, local(): jnp.einsum('kh,dhc->kdc', hidden_group, hyper_out, preferred_element_type...  28 us
    all_gather x1, waiting for transfers between devices, local(): dl_all = lax.all_gather(dlogits, everyone, axis=0, tiled=True)  20.6 us
    all_to_all x1, blocking collectives, local(): lax.all_to_all(part.reshape(n_hyper, own * rows, classes), 'hyper', split...  11.8 us
    dot_general x1, matrix products, local(): jnp.einsum('kdc,dhc->kh', dheads, out_rows, preferred_element_type=f32)  7.1 us
  transfers between devices with their start and end apart: 3, of which 2 were waited for; matrix products, arithmetic and copies ran while one was open for 23% of the time, Pallas kernels for 0%

commit v1 on v0

--- a/solution.py
+++ b/solution.py
@@ -6,6 +6,27 @@
 highest = lax.Precision.HIGHEST
 f32 = jnp.float32
 bf16 = jnp.bfloat16
+
+
+def joined_along(pieces, dim):
+    shape = list(pieces.shape[1:])
+    shape[dim] *= pieces.shape[0]
+    return jnp.moveaxis(pieces, 0, dim).reshape(shape)
+
+
+def doubled(value, axis):
+    count, index = (lax.axis_size(axis), lax.axis_index(axis))
+    blocks, bit = (value[None], 1)
+    while bit < count:
+        other = lax.ppermute(blocks, axis, [(i, i ^ bit) for i in range(count)])
+        low = index & bit == 0
+        blocks = jnp.concatenate([jnp.where(low, blocks, other), jnp.where(low, other, blocks)])
+        bit *= 2
+    return blocks
+
+
+def collect(x, axis, dim):
+    return joined_along(doubled(x, axis), dim)
 
 
 def silu_slope(values):
@@ -36,7 +57,7 @@
     classes = hyper_out.shape[2]
     ids = lax.all_gather(client_ids, everyone, axis=0, tiled=True)
     in_group = lax.all_gather(inputs, "hyper", axis=0, tiled=True)
-    in_all = lax.all_gather(in_group, "dp", axis=0, tiled=True)
+    in_all = collect(in_group, "dp", 0)
     select = ids[:, None] == jnp.arange(embeddings.shape[0], dtype=jnp.int32)[None, :]
     picked = jnp.dot(select.astype(bf16), embeddings, preferred_element_type=f32).astype(bf16)
     hyper_preact = jnp.dot(picked, hyper_in, preferred_element_type=f32) + hyper_bias

time: 277 us -> 262 us (0.946)
  local copies, waits for them, and re-layouts: 42.4 us -> 25.6 us
  starting transfers between devices: 0.12 us -> 5.63 us
  matrix products: 61.7 us -> 58.7 us
    all_gather x1 -> x0, waiting for transfers between devices: 33.7 us -> none  [local(): in_all = lax.all_gather(in_group, 'dp', axis=0, tiled=True)]
    ppermute x0 -> x3, waiting for transfers between devices: none -> 22.5 us  [doubled(): other = lax.ppermute(blocks, axis, [(i, i ^ bit) for i in range(count)])]
    unnamed x16 -> x22, local copies, waits for them, and re-layouts: 33.5 us -> 12.1 us
    all_gather x1, waiting for transfers between devices: 20.6 us -> 29.9 us  [local(): dl_all = lax.all_gather(dlogits, everyone, axis=0, tiled=True)]
    dot_general x1, matrix products: 7.1 us -> 1.26 us  [local(): jnp.einsum('kdc,dhc->kh', dheads, out_rows, preferred_element_type=f32)]
    ppermute x0 -> x3, starting transfers between devices: none -> 5.55 us  [doubled(): other = lax.ppermute(blocks, axis, [(i, i ^ bit) for i in range(count)])]
    convert_element_type x2 -> x1, local copies, waits for them, and re-layouts: 4.08 us -> 6.54 us  [local(): jnp.einsum('krd,krc->kdc', features, dl_all, preferred_element_type=f32)]
  transfers between devices with their start and end apart: 3 -> 5, of which waited for: 2 -> 4; matrix products, arithmetic and copies ran while one was open for 23% -> 15% of each run, Pallas kernels for 0% -> 0%
where the time goes in v1:
time: 262 us; the launch traced here: 261 us
  blocking collectives  100 us (38%)
  matrix products  58.7 us (22%)
  waiting for transfers between devices  52.5 us (20%)
  local copies, waits for them, and re-layouts  25.6 us (10%)
  between operations  14.2 us (5%)
  starting transfers between devices  5.63 us (2%)
  other arithmetic  4.11 us (2%)
    unnamed x1, blocking collectives  42 us
    psum x1, blocking collectives, local(): dhidden = lax.psum(dhidden, everyone)  40.4 us
    all_gather x1, waiting for transfers between devices, local(): dl_all = lax.all_gather(dlogits, everyone, axis=0, tiled=True)  29.9 us
    dot_general x1, matrix products, local(): jnp.einsum('kh,dhc->kdc', hidden_group, hyper_out, preferred_element_type...  27.9 us
    ppermute x3, waiting for transfers between devices, doubled(): other = lax.ppermute(blocks, axis, [(i, i ^ bit) for i in range(count)])  22.5 us
    unnamed x22, local copies, waits for them, and re-layouts  12.1 us
    all_to_all x1, blocking collectives, local(): lax.all_to_all(part.reshape(n_hyper, own * rows, classes), 'hyper', split...  11.8 us
    convert_element_type x1, local copies, waits for them, and re-layouts, local(): jnp.einsum('krd,krc->kdc', features, dl_all, preferred_element_type=f32)  6.54 us
  transfers between devices with their start and end apart: 5, of which 4 were waited for; matrix products, arithmetic and copies ran while one was open for 15% of the time, Pallas kernels for 0%

profile of v1, /device:TPU:0, one launch (start us, length us, event | category | flops | bytes accessed | tf_op | source)
XLA Modules:
  0.0 260.9 jit_solution(16603999730346661471)
XLA Ops:
  7.2 0.9 dynamic-update-slice
  8.2 42.0 %all-reduce = s32[64]{0:T(128)S(1)} all-reduce(s32[64]{0:T(128)S(1)} %dynamic-update-slice), channel_id=1, replica_groups=mesh['dp'=8,'hyper'=4] {'dp','hyper'}, use_global_device_ids=true, to_apply=%add | all-reduce | flops 64 | bytes 512
  50.1 6.0 %all_gather.12 = bf16[8,64,128]{2,1,0:T(8,128)(2,1)S(1)} all-gather(bf16[2,64,128]{2,1,0:T(8,128)(2,1)} %param.9), channel_id=1, replica_groups=mesh['dp'=8,'hyper'=4] {'hyper'}, dimensions={0}, use_global_device_ids=true | all-gather | bytes 163840 | tf_op jit(solution)/shard_map/all_gather | solution.py:59
  56.8 0.9 convolution_convert_fusion.1
  57.7 0.9 multiply_convert_fusion.2
  58.6 1.7 fusion.15
  60.3 27.9 %fusion = bf16[8,1024,256]{2,0,1:T(8,128)(2,1)S(1)} fusion(bf16[1024,50,256]{2,0,1:T(8,128)(2,1)} %param.17, bf16[64,50]{0,1:T(8,128)(2,1)S(1)} %get-tuple-element.29, s32[]{:T(128)S(6)} %select_n.60), kind=kOutput, calls=%fused_computation | convolution fusion | flops 209715200 | bytes 30415108 | tf_op jit(solution)/shard_map/kh,dhc->kdc/dot_general | solution.py:70
  88.2 2.1 fusion.2
  90.3 11.8 %all_to_all.5 = f32[4,128,256]{2,1,0:T(8,128)S(1)} all-to-all(f32[4,128,256]{2,1,0:T(8,128)S(1)} %bitcast.64), channel_id=1, replica_groups=mesh['dp'=8,'hyper'=4] {'hyper'}, dimensions={0} | all-to-all | bytes 1048576 | tf_op jit(solution)/shard_map/all_to_all | solution.py:72
  102.6 0.8 multiply_convert_fusion.1
  103.4 1.4 collective-permute-start
  104.8 3.6 %collective-permute-done = bf16[1,8,64,128]{3,2,1,0:T(8,128)(2,1)S(1)} collective-permute-done((bf16[1,8,64,128]{3,2,1,0:T(8,128)(2,1)S(1)}, bf16[1,8,64,128]{3,2,1,0:T(8,128)(2,1)S(1)}, u32[]{:S(2)}, u32[]{:S(2)}) %collective-permute-start) | collective-permute-done | bytes 131104 | tf_op jit(solution)/shard_map/ppermute | solution.py:21
  108.5 1.6 collective-permute-start.1
  110.1 2.2 constant_dynamic-slice_fusion
  112.3 3.3 %collective-permute-done.1 = bf16[2,8,64,128]{3,2,1,0:T(8,128)(2,1)S(1)} collective-permute-done((bf16[2,8,64,128]{3,2,1,0:T(8,128)(2,1)S(1)}, bf16[2,8,64,128]{3,2,1,0:T(8,128)(2,1)S(1)}, u32[]{:S(2)}, u32[]{:S(2)}) %collective-permute-start.1) | collective-permute-done | bytes 262176 | tf_op jit(solution)/shard_map/ppermute | solution.py:21
  115.7 2.6 collective-permute-start.2
  119.0 5.1 %fusion.6 = bf16[64,128,256]{2,0,1:T(8,128)(2,1)} fusion(bf16[128,50,256]{2,0,1:T(8,128)(2,1)S(1)} %constant_dynamic-slice_fusion, bf16[64,50]{0,1:T(8,128)(2,1)S(1)} %get-tuple-element.29), kind=kOutput, calls=%fused_computation.9 | convolution fusion | flops 209715200 | bytes 7477504 | tf_op jit(solution)/shard_map/kh,dhc->kdc/dot_general | solution.py:85
  124.1 15.6 %collective-permute-done.2 = bf16[4,8,64,128]{3,2,1,0:T(8,128)(2,1)S(1)} collective-permute-done((bf16[4,8,64,128]{3,2,1,0:T(8,128)(2,1)S(1)}, bf16[4,8,64,128]{3,2,1,0:T(8,128)(2,1)S(1)}, u32[]{:S(2)}, u32[]{:S(2)}) %collective-permute-start.2) | collective-permute-done | bytes 524320 | tf_op jit(solution)/shard_map/ppermute | solution.py:21
  139.9 29.9 %all-gather.3.cloned.1.call-done = bf16[64,64,256]{2,1,0:T(8,128)(2,1)} async-done(((bf16[2,64,256]{2,1,0:T(8,128)(2,1)}), bf16[64,64,256]{2,1,0:T(8,128)(2,1)}) %all-gather.3.cloned.1.call-update) | async-done | bytes 2097168 | tf_op jit(solution)/shard_map/all_gather | solution.py:77
  169.8 5.5 %fusion.16 = bf16[64,64,128]{2,1,0:T(8,128)(2,1)S(1)} fusion(bf16[64,64,256]{2,1,0:T(8,128)(2,1)} %all-gather.3.cloned.1.call-done, bf16[64,128,256]{2,0,1:T(8,128)(2,1)} %fusion.6), kind=kOutput, calls=%fused_computation.24 | convolution fusion | flops 268959744 | bytes 7340032 | tf_op jit(solution)/shard_map/krc,kdc->krd/dot_general | solution.py:87
  175.3 2.3 convert_reduce_fusion
  178.8 6.4 %copy.27 = bf16[128,50,256]{0,1,2:T(8,128)(2,1)} copy(bf16[128,50,256]{2,0,1:T(8,128)(2,1)} %copy-done.2) | data formatting | bytes 6553600
  185.2 3.3 %convolution_convert_fusion = bf16[64,128,256]{2,1,0:T(8,128)(2,1)} fusion(bf16[64,64,128]{2,1,0:T(8,128)(2,1)S(1)} %bitcast.61, bf16[64,64,256]{2,1,0:T(8,128)(2,1)S(1)} %copy-done.5), kind=kOutput, calls=%fused_computation.12 | convolution fusion | flops 270532608 | bytes 7340032 | tf_op jit(solution)/shard_map/krd,krc->kdc/dot_general | solution.py:86
  188.5 6.5 %copy.20 = bf16[64,128,256]{1,0,2:T(8,128)(2,1)} copy(bf16[64,128,256]{2,1,0:T(8,128)(2,1)} %convolution_convert_fusion) | data formatting | bytes 8388608 | tf_op jit(solution)/shard_map/convert_element_type | solution.py:86
  195.0 5.4 %fusion.8 = f32[128,50,256]{2,1,0:T(8,128)S(1)} fusion(bf16[64,128,256]{2,1,0:T(8,128)(2,1)} %convolution_convert_fusion, bf16[64,50]{0,1:T(8,128)(2,1)S(1)} %get-tuple-element.29), kind=kOutput, calls=%fused_computation.11 | convolution fusion | flops 209715200 | bytes 10754304 | tf_op jit(solution)/shard_map/kh,kdc->dhc/dot_general | solution.py:93
  200.5 4.8 %copy.22 = f32[128,50,256]{2,0,1:T(8,128)} copy(f32[128,50,256]{2,1,0:T(8,128)S(1)} %fusion.8) | data formatting | bytes 13107200
  205.3 1.3 convolution_bitcast_fusion
  206.5 40.4 %psum.7 = f32[64,50]{0,1:T(8,128)S(1)} all-reduce(f32[64,50]{0,1:T(8,128)S(1)} %convolution_bitcast_fusion), channel_id=1, replica_groups=mesh['dp'=8,'hyper'=4] {'dp','hyper'}, use_global_device_ids=true, to_apply=%region_4.5 | all-reduce | flops 3200 | bytes 25600 | tf_op jit(solution)/shard_map/psum | solution.py:95
  247.8 0.9 fusion.19
  248.7 0.8 fusion.33
  249.5 1.5 slice.9
  251.0 3.1 %slice.8 = f32[128,4096]{1,0:T(8,128)} slice(f32[129,4096]{1,0:T(8,128)} %all-gather.5.cloned.1.call-done), slice={[0:128], [0:4096]} | slice | bytes 4194304 | tf_op jit(solution)/shard_map/slice | solution.py:103
  (41 shorter events, 4.4 us)
Async XLA Ops:
  7.2 51.5 %copy-start = (bf16[128,4096]{1,0:T(8,128)(2,1)S(1)}, bf16[128,4096]{1,0:T(8,128)(2,1)}, u32[]{:S(2)}) copy-start(bf16[128,4096]{1,0:T(8,128)(2,1)} %param.12) | copy-start | bytes 3145732
  7.2 162.6 %all-gather.3.cloned.1.call-start = ((), (), s32[]{:S(2)}) async-start(), calls=%async_computation.1 | async-start | bytes 2162688 | tf_op jit(solution)/shard_map/all_gather | solution.py:77
  88.2 14.4 %copy-start.8 = (s32[2,64]{1,0:T(2,128)S(1)}, s32[2,64]{1,0:T(2,128)}, u32[]{:S(2)}) copy-start(s32[2,64]{1,0:T(2,128)} %param.10) | copy-start | bytes 1540
  103.4 146.1 %all-gather.5.cloned.1.call-start = ((), (), s32[]{:S(2)}) async-start(), calls=%async_computation.2 | async-start | bytes 2297856 | tf_op jit(solution)/shard_map/all_gather | solution.py:102
  103.4 5.0 %collective-permute-start = (bf16[1,8,64,128]{3,2,1,0:T(8,128)(2,1)S(1)}, bf16[1,8,64,128]{3,2,1,0:T(8,128)(2,1)S(1)}, u32[]{:S(2)}, u32[]{:S(2)}) collective-permute-start(bf16[1,8,64,128]{3,2,1,0:T(8,128)(2,1)S(1)} %bitcast.63), channel_id=1, source_target_pairs={{0,4},{4,0},{8,12},{12,8},{16,20},{20,16},{24,28},{28,24},{1,5},{5... | collective-permute-start | bytes 393224 | tf_op jit(solution)/shard_map/ppermute | solution.py:21
  108.5 7.0 %collective-permute-start.1 = (bf16[2,8,64,128]{3,2,1,0:T(8,128)(2,1)S(1)}, bf16[2,8,64,128]{3,2,1,0:T(8,128)(2,1)S(1)}, u32[]{:S(2)}, u32[]{:S(2)}) collective-permute-start(bf16[2,8,64,128]{3,2,1,0:T(8,128)(2,1)S(1)} %pad_maximum_fusion.2), channel_id=1, source_target_pairs={{0,8},{4,12},{8,0},{12,4},{16,24},{20,28},{24,16},{28,20},{1,9},{5... | collective-permute-start | bytes 786440 | tf_op jit(solution)/shard_map/ppermute | solution.py:21
  112.3 11.8 %copy-start.2 = (bf16[128,50,256]{2,0,1:T(8,128)(2,1)}, bf16[128,50,256]{2,0,1:T(8,128)(2,1)S(1)}, u32[]{:S(2)}) copy-start(bf16[128,50,256]{2,0,1:T(8,128)(2,1)S(1)} %constant_dynamic-slice_fusion) | copy-start | bytes 9830404
  115.7 24.0 %collective-permute-start.2 = (bf16[4,8,64,128]{3,2,1,0:T(8,128)(2,1)S(1)}, bf16[4,8,64,128]{3,2,1,0:T(8,128)(2,1)S(1)}, u32[]{:S(2)}, u32[]{:S(2)}) collective-permute-start(bf16[4,8,64,128]{3,2,1,0:T(8,128)(2,1)S(1)} %pad_maximum_fusion.1), channel_id=1, source_target_pairs={{0,16},{4,20},{8,24},{12,28},{16,0},{20,4},{24,8},{28,12},{1,17},{... | collective-permute-start | bytes 1572872 | tf_op jit(solution)/shard_map/ppermute | solution.py:21
  178.8 6.4 %copy-start.5 = (bf16[64,64,256]{2,1,0:T(8,128)(2,1)S(1)}, bf16[64,64,256]{2,1,0:T(8,128)(2,1)}, u32[]{:S(2)}) copy-start(bf16[64,64,256]{2,1,0:T(8,128)(2,1)} %all-gather.3.cloned.1.call-done) | copy-start | bytes 6291460
  178.8 6.4 %copy-start.6 = (bf16[4096,128]{1,0:T(8,128)(2,1)S(1)}, bf16[4096,128]{1,0:T(8,128)(2,1)}, u32[]{:S(2)}) copy-start(bf16[4096,128]{1,0:T(8,128)(2,1)} %get-tuple-element.22) | copy-start | bytes 3145732
  200.5 4.8 %copy-start.3 = (bf16[64,128,256]{1,0,2:T(8,128)(2,1)S(1)}, bf16[64,128,256]{1,0,2:T(8,128)(2,1)}, u32[]{:S(2)}) copy-start(bf16[64,128,256]{1,0,2:T(8,128)(2,1)} %copy.20) | copy-start | bytes 12582916
  200.5 4.8 %copy-start.4 = (bf16[128,50,256]{0,1,2:T(8,128)(2,1)S(1)}, bf16[128,50,256]{0,1,2:T(8,128)(2,1)}, u32[]{:S(2)}) copy-start(bf16[128,50,256]{0,1,2:T(8,128)(2,1)} %copy.27) | copy-start | bytes 9830404
  205.3 42.3 %copy-start.7 = (bf16[128,50]{0,1:T(8,128)(2,1)S(1)}, bf16[128,50]{0,1:T(8,128)(2,1)}, u32[]{:S(2)}) copy-start(bf16[128,50]{0,1:T(8,128)(2,1)} %param.15) | copy-start | bytes 38404
  205.3 48.8 %copy-start.1 = (bf16[128,4096]{1,0:T(8,128)(2,1)S(1)}, bf16[128,4096]{1,0:T(8,128)(2,1)}, u32[]{:S(2)}) copy-start(bf16[128,4096]{1,0:T(8,128)(2,1)} %param.12) | copy-start | bytes 3145732
Sparse Core Ops, SparseCore 0:
  103.5 66.2 all-gather.2
  178.9 56.6 all-gather.4
